TPU v7x, 32 devices: a whole 2x2x4 slice. The times are simulated.
32 devices in a mesh: img: 4 (over y, core), txt: 8 (over z, x).
Axes of the slice: x: 2, y: 2, z: 4, core: 2. Of those that a mesh axis runs over, the one named last changes fastest.
Arguments:
- queries: bfloat16 [1, 5120, 8192], P(None, 'txt', 'img'), may hold values from -128 to 128
- visual_keys: bfloat16 [1, 512, 8192], P(None, 'img'), may hold values from -5 to 5
- visual_values: bfloat16 [1, 512, 8192], P(None, 'img'), may hold values from -6 to 6
- out_grad: bfloat16 [1, 5120, 8192], P(None, 'txt', 'img'), may hold values from -6 to 6
- gate_value: float32 [1, 64], P(None, 'img'), may hold values from -1.5 to 1.5
- image_order: int32 [1, 8], replicated, may hold values from 0 to 7, as said below
- image_seen: int32 [5120], P('txt'), may hold values from 1 to 8
Outputs:
- query_grad: bfloat16 [1, 5120, 8192], P(None, 'txt', 'img')
- key_grad: float32 [1, 512, 8192], P(None, 'txt', 'img')
- value_grad: float32 [1, 512, 8192], P(None, 'txt', 'img')
Inputs may be any that keep to these rules, and one draw needn't show every extreme that they name: `image_order`: each row names every image of 0 to 7 once.
All inputs are finite; a program needn't handle non-finite values.
Results may differ from a plain program's by a relative error of at most 0.0058.
Values may be sent and summed in bfloat16 or wider, within the bound.
A program may use at most 128 MiB of HBM per device.

v0:
```python
import math

import jax
import jax.numpy as jnp
from jax import lax
from jax.sharding import PartitionSpec as P


def image_mask(order_row, image_seen, key_count):
    image_count = order_row.shape[0]
    latent_count = key_count // image_count
    key_image = jnp.broadcast_to(order_row[:, None], (image_count, latent_count)).reshape(key_count)
    return key_image[None, :] < image_seen[:, None]


def attention_grads(query, grad_in, factor, key_rows, value_rows, allowed, score_scale):
    token_count = query.shape[0]
    head_count = factor.shape[0]
    head_width = query.shape[1] // head_count
    key_count = key_rows.shape[0]
    query_heads = query.reshape(token_count, head_count, head_width)
    key_heads = key_rows.reshape(key_count, head_count, head_width)
    value_heads = value_rows.reshape(key_count, head_count, head_width)
    gated_grad = (
        grad_in.reshape(token_count, head_count, head_width).astype(jnp.float32)
        * factor[None, :, None]
    ).astype(jnp.bfloat16)
    scores = (
        jnp.einsum("thd,khd->htk", query_heads, key_heads, preferred_element_type=jnp.float32)
        * score_scale
    )
    masked = jnp.where(allowed[None], scores, -1e30)
    row_max = jnp.max(masked, axis=2, keepdims=True)
    exponent = jnp.where(allowed[None], jnp.exp(masked - row_max), 0.0)
    weights = exponent / jnp.sum(exponent, axis=2, keepdims=True)
    weight_half = weights.astype(jnp.bfloat16)
    attended = jnp.einsum(
        "htk,khd->thd", weight_half, value_heads, preferred_element_type=jnp.float32
    )
    row_delta = jnp.sum(gated_grad.astype(jnp.float32) * attended, axis=2)
    weight_grad = jnp.einsum(
        "thd,khd->htk", gated_grad, value_heads, preferred_element_type=jnp.float32
    )
    score_half = (weights * (weight_grad - jnp.transpose(row_delta)[:, :, None])).astype(
        jnp.bfloat16
    )
    query_part = (
        jnp.einsum("htk,khd->thd", score_half, key_heads, preferred_element_type=jnp.float32)
        * score_scale
    )
    return (
        query_part.astype(jnp.bfloat16).reshape(token_count, -1),
        score_half,
        weight_half,
        query_heads,
        gated_grad,
    )


def latent_terms(score_half, weight_half, query_heads, gated_grad, count, score_scale):
    key_part = (
        jnp.einsum("htk,thd->khd", score_half, query_heads, preferred_element_type=jnp.float32)
        * score_scale
    )
    value_part = jnp.einsum(
        "htk,thd->khd", weight_half, gated_grad, preferred_element_type=jnp.float32
    )
    return (key_part.reshape(count, -1), value_part.reshape(count, -1))


def shards(queries, visual_keys, visual_values, out_grad, gate_value, image_order, image_seen):
    width_local = queries.shape[2]
    head_width = width_local // gate_value.shape[1]
    score_scale = 1.0 / math.sqrt(head_width)
    key_rows = lax.all_to_all(visual_keys[0], "img", split_axis=1, concat_axis=0, tiled=True)
    value_rows = lax.all_to_all(visual_values[0], "img", split_axis=1, concat_axis=0, tiled=True)
    key_total = key_rows.shape[0]
    allowed = image_mask(image_order[0], image_seen, key_total)
    factor = jnp.tanh(gate_value[0])
    query_part, score_half, weight_half, query_heads, gated_grad = attention_grads(
        queries[0], out_grad[0], factor, key_rows, value_rows, allowed, score_scale
    )
    query_list = [query_part]
    key_part, value_part = latent_terms(
        score_half, weight_half, query_heads, gated_grad, key_total, score_scale
    )
    key_share = lax.psum_scatter(key_part, "txt", scatter_dimension=0, tiled=True)
    value_share = lax.psum_scatter(value_part, "txt", scatter_dimension=0, tiled=True)
    key_list = [key_share]
    value_list = [value_share]
    key_grad = jnp.stack(key_list)
    value_grad = jnp.stack(value_list)
    return (jnp.stack(query_list), key_grad, value_grad)


def solution(mesh):
    placed = (
        P(None, "txt", "img"),
        P(None, "img", None),
        P(None, "img", None),
        P(None, "txt", "img"),
        P(None, "img"),
        P(),
        P("txt"),
    )
    return jax.shard_map(
        shards,
        mesh=mesh,
        in_specs=placed,
        out_specs=(P(None, "txt", "img"), P(None, "txt", "img"), P(None, "txt", "img")),
        check_vma=False,
    )
```

profile of v0, /device:TPU:0, one launch (start us, length us, event | category | flops | bytes accessed | tf_op | source)
XLA Modules:
  0.0 274.3 jit_solution(15759420821382776960)
XLA Ops:
  7.2 3.3 %all_to_all.24 = bf16[128,4,2048]{2,1,0:T(4,128)(2,1)S(1)} reshape(bf16[1,128,8192]{2,1,0:T(8,128)(2,1)} %param.8) | data formatting | bytes 4194304 | tf_op jit(solution)/shard_map/all_to_all | solution.py:75
  13.0 4.7 %all-to-all-start = ((bf16[128,4,2048]{2,0,1:T(8,128)(2,1)}), bf16[128,4,2048]{2,0,1:T(8,128)(2,1)}, u32[]{:S(2)}, u32[]{:S(2)}) async-start(bf16[128,4,2048]{2,0,1:T(8,128)(2,1)} %copy.24), calls=%async_computation | async-start | bytes 4194304 | tf_op jit(solution)/shard_map/all_to_all | solution.py:75
  18.0 2.6 copy.48
  20.5 4.9 %copy.27 = f32[1,640,2048]{1,2,0:T(8,128)} copy(bf16[1,640,2048]{2,1,0:T(8,128)(2,1)} %param.10) | data formatting | bytes 7864320 | tf_op jit(solution)/shard_map/convert_element_type | solution.py:25
  25.7 3.1 %multiply_convert_fusion.2 = bf16[640,16,128]{0,2,1:T(8,128)(2,1)S(1)} fusion(f32[640,16,128]{0,2,1:T(8,128)} %bitcast.43, f32[16]{0:T(128)S(1)} %tanh_bitcast_fusion), kind=kLoop, calls=%fused_computation.13 | loop fusion | flops 2621440 | bytes 7864384 | tf_op jit(solution)/shard_map/convert_element_type | solution.py:27
  28.8 15.4 %all-to-all-done = bf16[128,4,2048]{2,0,1:T(8,128)(2,1)} async-done(((bf16[128,4,2048]{2,0,1:T(8,128)(2,1)}), bf16[128,4,2048]{2,0,1:T(8,128)(2,1)}, u32[]{:S(2)}, u32[]{:S(2)}) %all-to-all-start) | async-done | bytes 2097184 | tf_op jit(solution)/shard_map/all_to_all | solution.py:75
  44.2 3.6 %copy.49 = bf16[64,8,16,128]{3,2,1,0:T(8,128)(2,1)} copy(bf16[64,8,16,128]{3,1,2,0:T(8,128)(2,1)} %bitcast.20) | data formatting | bytes 4194304
  47.8 4.3 %copy.35 = bf16[512,16,128]{0,2,1:T(8,128)(2,1)} copy(bf16[512,16,128]{2,1,0:T(8,128)(2,1)} %bitcast.49) | data formatting | bytes 4194304 | tf_op jit(solution)/shard_map/reshape | solution.py:22
  52.1 14.4 %fusion.11 = (f32[16,640]{1,0:T(8,128)S(1)}, f32[16,640,512]{1,2,0:T(8,128)}) fusion(pred[640,512]{0,1:T(8,128)(4,1)S(1)} %broadcast_compare_fusion, bf16[640,16,128]{0,2,1:T(8,128)(2,1)} %bitcast.47, bf16[512,16,128]{0,2,1:T(8,128)(2,1)} %copy.35), kind=kOutput, calls=%fused_computation.20 | convolution fusion | flops 1368392192 | bytes 26058752 | tf_op jit(solution)/shard_map/sub | solution.py:34
  66.4 8.5 %fusion.5 = bf16[16,640,512]{1,2,0:T(8,128)(2,1)S(1)} fusion(f32[16,640,512]{1,2,0:T(8,128)} %get-tuple-element.10, f32[16,640]{1,0:T(8,128)S(1)} %get-tuple-element.9), kind=kLoop, calls=%fused_computation.9 | loop fusion | flops 10485760 | bytes 31498240 | tf_op jit(solution)/shard_map/convert_element_type | solution.py:36
  75.0 5.3 %fusion.12 = f32[16,128,512]{2,1,0:T(8,128)} fusion(bf16[640,16,128]{0,2,1:T(8,128)(2,1)S(1)} %multiply_convert_fusion.2, bf16[16,640,512]{1,2,0:T(8,128)(2,1)S(1)} %fusion.5), kind=kOutput, calls=%fused_computation.21 | convolution fusion | flops 1342177280 | bytes 17301504 | tf_op jit(solution)/shard_map/htk,thd->khd/dot_general | solution.py:65
  80.3 5.4 %copy.40 = f32[512,2048]{1,0:T(8,128)} copy(f32[512,2048]{0,1:T(8,128)} %bitcast.46) | data formatting | bytes 8388608 | tf_op jit(solution)/shard_map/reshape | solution.py:68
  86.0 4.5 %all_to_all.27 = bf16[128,4,2048]{2,1,0:T(4,128)(2,1)} reshape(bf16[1,128,8192]{2,1,0:T(8,128)(2,1)} %param.9) | data formatting | bytes 4194304 | tf_op jit(solution)/shard_map/all_to_all | solution.py:76
  90.5 2.7 %copy.28 = bf16[128,4,2048]{2,0,1:T(8,128)(2,1)S(1)} copy(bf16[128,4,2048]{2,1,0:T(4,128)(2,1)} %all_to_all.27) | data formatting | bytes 4194304 | tf_op jit(solution)/shard_map/all_to_all | solution.py:76
  93.3 28.1 %all_to_all.32 = bf16[128,4,2048]{2,0,1:T(8,128)(2,1)S(1)} all-to-all(bf16[128,4,2048]{2,0,1:T(8,128)(2,1)S(1)} %copy.28), channel_id=1, replica_groups=mesh['img'=4,'txt'=8] {'img'}, dimensions={1} | all-to-all | bytes 4194304 | tf_op jit(solution)/shard_map/all_to_all | solution.py:76
  123.3 4.3 %copy.32 = bf16[512,16,128]{0,2,1:T(8,128)(2,1)} copy(bf16[512,16,128]{2,1,0:T(8,128)(2,1)} %bitcast.51) | data formatting | bytes 4194304 | tf_op jit(solution)/shard_map/reshape | solution.py:23
  127.7 6.8 %fusion.6 = f32[640,16]{0,1:T(8,128)S(1)} fusion(bf16[640,16,128]{0,2,1:T(8,128)(2,1)S(1)} %multiply_convert_fusion.2, bf16[512,16,128]{0,2,1:T(8,128)(2,1)} %copy.32, bf16[16,640,512]{1,2,0:T(8,128)(2,1)} %copy-done), kind=kOutput, calls=%fused_computation.11 | convolution fusion | flops 1346099200 | bytes 15245312 | tf_op jit(solution)/shard_map/htk,khd->thd/dot_general | solution.py:37
  134.5 12.5 %multiply_convert_fusion = bf16[16,640,512]{1,2,0:T(8,128)(2,1)} fusion(f32[16,640]{1,0:T(8,128)S(1)} %bitcast.52, f32[16,640,512]{1,2,0:T(8,128)} %get-tuple-element.10, f32[16,640]{1,0:T(8,128)S(1)} %get-tuple-element.9, bf16[512,16,128]{0,2,1:T(8,128)(2,1)S(1)} %copy-done.1, bf16[640,16,128]{0,2,1:T(8,128)(2,1)S(1)} %multiply_convert_fusion.2), kind=kOutput, calls=%fused_computation.1 | convolution fusion | flops 1363148800 | bytes 36257792 | tf_op jit(solution)/shard_map/thd,khd->htk/dot_general | solution.py:41
  147.0 10.1 %broadcast_multiply_fusion = f32[16,512,128]{1,2,0:T(8,128)} fusion(bf16[16,640,512]{1,2,0:T(8,128)(2,1)} %multiply_convert_fusion, bf16[640,16,128]{0,2,1:T(8,128)(2,1)} %bitcast.48), kind=kOutput, calls=%fused_computation.14 | convolution fusion | flops 1343225856 | bytes 17301504 | tf_op jit(solution)/shard_map/htk,thd->khd/dot_general | solution.py:62
  157.0 5.4 %copy.38 = f32[512,2048]{1,0:T(8,128)} copy(f32[512,2048]{0,1:T(8,128)} %bitcast.45) | data formatting | bytes 8388608 | tf_op jit(solution)/shard_map/reshape | solution.py:68
  162.5 6.6 %multiply_convert_fusion.1 = bf16[16,640,128]{1,2,0:T(8,128)(2,1)S(1)} fusion(bf16[512,16,128]{0,2,1:T(8,128)(2,1)} %copy.35, bf16[16,640,512]{1,2,0:T(8,128)(2,1)} %multiply_convert_fusion), kind=kOutput, calls=%fused_computation.12 | convolution fusion | flops 1344798720 | bytes 15204352 | tf_op jit(solution)/shard_map/htk,khd->thd/dot_general | solution.py:48
  169.1 2.6 copy.41
  171.7 3.6 %reduce-scatter.5.cloned.1.call-done = f32[64,2048]{1,0:T(8,128)} async-done(((f32[512,2048]{1,0:T(8,128)}), f32[64,2048]{1,0:T(8,128)}) %reduce-scatter.5.cloned.1.call-update) | async-done | bytes 524304 | tf_op jit(solution)/shard_map/reduce_scatter | solution.py:88
  175.3 92.2 %reduce-scatter.3.cloned.1.call-done = f32[64,2048]{1,0:T(8,128)} async-done(((f32[512,2048]{1,0:T(8,128)}), f32[64,2048]{1,0:T(8,128)}) %reduce-scatter.3.cloned.1.call-update) | async-done | bytes 524304 | tf_op jit(solution)/shard_map/reduce_scatter | solution.py:87
  (22 shorter events, 5.2 us)
Async XLA Ops:
  10.5 7.3 %copy-start.4 = (s32[1,8]{1,0:T(1,128)S(1)}, s32[1,8]{1,0:T(1,128)}, u32[]{:S(2)}) copy-start(s32[1,8]{1,0:T(1,128)} %param.12) | copy-start | bytes 100
  13.0 4.9 %copy-start.2 = (bf16[1,640,2048]{2,1,0:T(8,128)(2,1)S(1)}, bf16[1,640,2048]{2,1,0:T(8,128)(2,1)}, u32[]{:S(2)}) copy-start(bf16[1,640,2048]{2,1,0:T(8,128)(2,1)} %param.7) | copy-start | bytes 7864324
  13.0 31.2 %all-to-all-start = ((bf16[128,4,2048]{2,0,1:T(8,128)(2,1)}), bf16[128,4,2048]{2,0,1:T(8,128)(2,1)}, u32[]{:S(2)}, u32[]{:S(2)}) async-start(bf16[128,4,2048]{2,0,1:T(8,128)(2,1)} %copy.24), calls=%async_computation | async-start | bytes 4194304 | tf_op jit(solution)/shard_map/all_to_all | solution.py:75
  17.8 157.5 %reduce-scatter.5.cloned.1.call-start = ((), (), s32[]{:S(2)}) async-start(), calls=%async_computation.5 | async-start | bytes 4718592 | tf_op jit(solution)/shard_map/reduce_scatter | solution.py:88
  20.5 4.9 %copy-start.5 = (f32[1,16]{1,0:T(1,128)S(1)}, f32[1,16]{1,0:T(1,128)}, u32[]{:S(2)}) copy-start(f32[1,16]{1,0:T(1,128)} %param.11) | copy-start | bytes 196
  20.5 4.9 %copy-start.3 = (s32[640]{0:T(1024)S(1)}, s32[640]{0:T(1024)}, u32[]{:S(2)}) copy-start(s32[640]{0:T(1024)} %param.13) | copy-start | bytes 7684
  75.0 5.3 %copy-start = (bf16[16,640,512]{1,2,0:T(8,128)(2,1)}, bf16[16,640,512]{1,2,0:T(8,128)(2,1)S(1)}, u32[]{:S(2)}) copy-start(bf16[16,640,512]{1,2,0:T(8,128)(2,1)S(1)} %fusion.5) | copy-start | bytes 31457284
  85.8 181.7 %reduce-scatter.3.cloned.1.call-start = ((), (), s32[]{:S(2)}) async-start(), calls=%async_computation.4 | async-start | bytes 4718592 | tf_op jit(solution)/shard_map/reduce_scatter | solution.py:87
  127.7 6.8 %copy-start.1 = (bf16[512,16,128]{0,2,1:T(8,128)(2,1)S(1)}, bf16[512,16,128]{0,2,1:T(8,128)(2,1)}, u32[]{:S(2)}) copy-start(bf16[512,16,128]{0,2,1:T(8,128)(2,1)} %copy.32) | copy-start | bytes 6291460
Sparse Core Ops, SparseCore 0:
  85.9 89.3 reduce-scatter.4
  179.5 87.9 reduce-scatter.2
where the time goes:
time: 275 us; the launch traced here: 274 us
  waiting for transfers between devices  111 us (40%)
  matrix products  55.7 us (20%)
  local copies, waits for them, and re-layouts  48.4 us (18%)
  blocking collectives  28.1 us (10%)
  between operations  14.1 us (5%)
  other arithmetic  11.9 us (4%)
  starting transfers between devices  4.98 us (2%)
    reduce_scatter x1, waiting for transfers between devices, shards(): lax.psum_scatter(key_part, 'txt', scatter_dimension=0, tiled=True)  92.2 us
    all_to_all x1, blocking collectives, shards(): lax.all_to_all(visual_values[0], 'img', split_axis=1, concat_axis=0, tile...  28.1 us
    all_to_all x1, waiting for transfers between devices, shards(): lax.all_to_all(visual_keys[0], 'img', split_axis=1, concat_axis=0, tiled=...  15.4 us
    sub x1, matrix products, attention_grads(): exponent = jnp.where(allowed[None], jnp.exp(masked - row_max), 0.0)  14.4 us
    dot_general x1, matrix products, attention_grads(): jnp.einsum('thd,khd->htk', gated_grad, value_heads, preferred_element_typ...  12.5 us
    reshape x2, local copies, waits for them, and re-layouts, latent_terms(): return (key_part.reshape(count, -1), value_part.reshape(count, -1))  10.8 us
    dot_general x1, matrix products, latent_terms(): jnp.einsum('htk,thd->khd', score_half, query_heads, preferred_element_typ...  10.1 us
    convert_element_type x1, other arithmetic, attention_grads(): weight_half = weights.astype(jnp.bfloat16)  8.53 us
  transfers between devices with their start and end apart: 3, of which 3 were waited for; matrix products, arithmetic and copies ran while one was open for 23% of the time, Pallas kernels for 0%

commit v1 on v0

v1 whole, which is shorter than its diff:
```python
import functools
import math

import jax
import jax.numpy as jnp
from jax import lax
from jax.experimental import pallas as pl
from jax.experimental.pallas import tpu as pltpu
from jax.sharding import PartitionSpec as P

NT = (((1,), (1,)), ((), ()))
TN = (((0,), (0,)), ((), ()))
NN = (((1,), (0,)), ((), ()))


def matmul(left, right, dims):
    return lax.dot_general(left, right, dims, preferred_element_type=jnp.float32)


def head_grads(query, gated, key, value, bias):
    rows, tokens = key.shape[0], query.shape[0]
    images = bias.shape[0]
    scale = 1.0 / math.sqrt(query.shape[1])
    scores = matmul(key, query, NT) * (scale * math.log2(math.e))
    masked = (scores.reshape(images, rows // images, tokens) + bias[:, None, :]).reshape(rows, tokens)
    exponent = jnp.exp2(masked - jnp.max(masked, axis=0, keepdims=True))
    weights = exponent * (1.0 / jnp.sum(exponent, axis=0, keepdims=True))
    weight_half = weights.astype(jnp.bfloat16)
    weight_grad = matmul(value, gated, NT)
    delta = jnp.sum(weight_half.astype(jnp.float32) * weight_grad, axis=0, keepdims=True)
    score_half = (weights * (weight_grad - delta)).astype(jnp.bfloat16)
    query_grad = (matmul(key, score_half, TN) * scale).T
    key_grad = matmul(score_half, query, NN) * scale
    value_grad = matmul(weight_half, gated, NN)
    return query_grad, key_grad, value_grad


def kernel(images_n, sides, order_ref, factor_ref, seen_ref, query_ref, grad_ref, key_ref, value_ref,
           out_ref, key_out, value_out,
           bias, latents, part, pair_out, pair_in, far_out, far_in,
           latent_send, latent_recv, pair_send, pair_recv, far_send, far_recv):
    head = pl.program_id(0)
    heads = pl.num_programs(0)
    width = query_ref.shape[1]
    owned = key_ref.shape[0]
    me = lax.axis_index("img")
    place = lax.axis_index("txt")
    mine = place // 2
    side = place % 2
    other = 1 - side
    partner = {"txt": mine * 2 + other}

    def latent_copy(source, index, slot, off):
        owner = (me + off) % images_n
        column = pl.multiple_of((owner * heads + index) * width, width)
        view = source.at[:, pl.ds(column, width)]
        target = latents.at[index, slot, pl.ds(pl.multiple_of(me * owned, owned), owned), :]
        if off == 0:
            return pltpu.make_async_copy(view, target, latent_recv.at[index])
        return pltpu.make_async_remote_copy(
            src_ref=view, dst_ref=target, send_sem=latent_send.at[index],
            recv_sem=latent_recv.at[index], device_id={"img": owner},
            device_id_type=pl.DeviceIdType.MESH)

    def pair_copy(index):
        return pltpu.make_async_remote_copy(
            src_ref=pair_out.at[index], dst_ref=pair_in.at[index],
            send_sem=pair_send.at[index], recv_sem=pair_recv.at[index],
            device_id=partner, device_id_type=pl.DeviceIdType.MESH)

    def far_copy(index, off):
        there = (mine + off) % sides
        return pltpu.make_async_remote_copy(
            src_ref=far_out.at[index, off - 1], dst_ref=far_in.at[index, off - 1],
            send_sem=far_send.at[index], recv_sem=far_recv.at[index],
            device_id={"txt": there * 2 + side}, device_id_type=pl.DeviceIdType.MESH)

    def drain(ref, sem):
        pltpu.make_async_copy(ref, ref, sem).wait()

    def columns(index):
        return pl.ds(pl.multiple_of(index * width, width), width)

    @pl.when(head == 0)
    def _():
        barrier = pltpu.get_barrier_semaphore()
        peers = [{"img": (me + off) % images_n} for off in range(1, images_n)] + [partner]
        peers += [{"txt": ((mine + off) % sides) * 2 + side} for off in range(1, sides)]
        for peer in peers:
            pl.semaphore_signal(barrier, inc=1, device_id=peer, device_id_type=pl.DeviceIdType.MESH)
        pl.semaphore_wait(barrier, len(peers))

        def send(index, carry):
            for off in list(range(1, images_n)) + [0]:
                latent_copy(key_ref, index, 0, off).start()
                latent_copy(value_ref, index, 1, off).start()
            return carry

        lax.fori_loop(0, heads, send, 0)
        for i in range(order_ref.shape[0]):
            bias[pl.ds(i, 1), :] = jnp.where(seen_ref[...] > order_ref[i], 0.0, -1e30)

    def relay(index):
        pair_copy(index).wait_recv()
        slot = index % 2
        for off in range(1, sides):
            there = (mine + off) % sides
            for kind in range(2):
                far_out[index, off - 1, kind] = (
                    part[slot, kind, there * 2 + side]
                    + pair_in[index, kind, there].astype(jnp.float32)
                ).astype(jnp.bfloat16)
        for off in range(1, sides):
            far_copy(index, off).start()
        for kind, out in enumerate((key_out, value_out)):
            out[:, columns(index)] = (
                part[slot, kind, mine * 2 + side] + pair_in[index, kind, mine].astype(jnp.float32)
            )

    def finish(index):
        drain(far_in.at[index], far_recv.at[index])
        for kind, out in enumerate((key_out, value_out)):
            total = out[:, columns(index)]
            for off in range(1, sides):
                total = total + far_in[index, off - 1, kind].astype(jnp.float32)
            out[:, columns(index)] = total

    drain(latents.at[head], latent_recv.at[head])
    gated = (grad_ref[...].astype(jnp.float32) * factor_ref[head]).astype(jnp.bfloat16)
    query_grad, key_grad, value_grad = head_grads(
        query_ref[...], gated, latents[head, 0], latents[head, 1], bias[...]
    )
    out_ref[...] = query_grad.astype(out_ref.dtype)
    now = head % 2
    shape = part.shape[2:]
    part[now, 0] = key_grad.reshape(shape)
    part[now, 1] = value_grad.reshape(shape)
    for kind in range(2):
        for there in range(sides):
            pair_out[head, kind, there] = part[now, kind, there * 2 + other].astype(jnp.bfloat16)
    pair_copy(head).start()

    @pl.when(head >= 1)
    def _():
        relay(head - 1)

    @pl.when(head >= 2)
    def _():
        finish(head - 2)

    @pl.when(head == heads - 1)
    def _():
        relay(heads - 1)
        finish(heads - 2)
        finish(heads - 1)

        def settle(index, carry):
            drain(latents.at[index, :, pl.ds(0, owned * (images_n - 1)), :], latent_send.at[index])
            pair_copy(index).wait_send()
            drain(far_out.at[index], far_send.at[index])
            return carry

        lax.fori_loop(0, heads, settle, 0)


def attention(images_n, texts_n, order, factor, seen, query, grad, key, value):
    tokens, width = query.shape
    heads = factor.shape[0]
    head_width = width // heads
    owned = key.shape[0]
    rows = owned * images_n
    sides = texts_n // 2
    share = rows // texts_n
    smem = pl.BlockSpec(memory_space=pltpu.SMEM)
    hbm = pl.BlockSpec(memory_space=pl.ANY)
    column = pl.BlockSpec((tokens, head_width), lambda h: (0, h))
    fixed = pl.BlockSpec((share, width), lambda h: (0, 0))
    half = jnp.bfloat16
    dma = pltpu.SemaphoreType.DMA((heads,))
    return pl.pallas_call(
        functools.partial(kernel, images_n, sides),
        grid=(heads,),
        in_specs=[smem, smem, pl.BlockSpec((1, tokens), lambda h: (0, 0)), column, column, hbm, hbm],
        out_specs=[column, fixed, fixed],
        out_shape=[jax.ShapeDtypeStruct((tokens, width), half)]
        + [jax.ShapeDtypeStruct((share, width), jnp.float32)] * 2,
        scratch_shapes=[
            pltpu.VMEM((order.shape[0], tokens), jnp.float32),
            pltpu.VMEM((heads, 2, rows, head_width), half),
            pltpu.VMEM((2, 2, texts_n, share, head_width), jnp.float32),
            pltpu.VMEM((heads, 2, sides, share, head_width), half),
            pltpu.VMEM((heads, 2, sides, share, head_width), half),
            pltpu.VMEM((heads, sides - 1, 2, share, head_width), half),
            pltpu.VMEM((heads, sides - 1, 2, share, head_width), half),
            dma, dma, dma, dma, dma, dma,
        ],
        compiler_params=pltpu.CompilerParams(
            vmem_limit_bytes=56 * 1024 * 1024, collective_id=0, has_side_effects=True
        ),
    )(order, factor, seen, query, grad, key, value)


def shards(images_n, texts_n, queries, visual_keys, visual_values, out_grad, gate_value, image_order, image_seen):
    factor = jnp.tanh(gate_value[0])
    query_grad, key_share, value_share = attention(
        images_n, texts_n, image_order[0], factor, image_seen[None, :],
        queries[0], out_grad[0], visual_keys[0], visual_values[0]
    )
    return (query_grad[None], key_share[None], value_share[None])


def solution(mesh):
    placed = (
        P(None, "txt", "img"),
        P(None, "img", None),
        P(None, "img", None),
        P(None, "txt", "img"),
        P(None, "img"),
        P(),
        P("txt"),
    )
    return jax.shard_map(
        functools.partial(shards, mesh.shape["img"], mesh.shape["txt"]),
        mesh=mesh,
        in_specs=placed,
        out_specs=(P(None, "txt", "img"), P(None, "txt", "img"), P(None, "txt", "img")),
        check_vma=False,
    )
```

time: 275 us -> 87.5 us (0.32)
  waiting for transfers between devices: 111 us -> 0 us
  Pallas kernels: 0 us -> 79 us
  matrix products: 55.7 us -> 0 us
  local copies, waits for them, and re-layouts: 48.4 us -> 7.68 us
  blocking collectives: 28.1 us -> 0 us
  between operations: 14.1 us -> 0.66 us
  other arithmetic: 11.9 us -> 0 us
  starting transfers between devices: 4.98 us -> 0 us
    reduce_scatter x2 -> x0, waiting for transfers between devices: 95.8 us -> none  [the longest x1 92.2 us: shards(): lax.psum_scatter(key_part, 'txt', scatter_dimension=0, tiled=True)]
    pallas_call x0 -> x1, Pallas kernels: none -> 79 us  [attention(): pl.pallas_call(functools.partial(kernel, images_n, sides), grid=(heads,),...]
    dot_general x5 -> x0, matrix products: 41.3 us -> none  [the longest x1 12.5 us: attention_grads(): jnp.einsum('thd,khd->htk', gated_grad, value_heads, preferred_element_typ...]
    all_to_all x1 -> x0, blocking collectives: 28.1 us -> none  [shards(): lax.all_to_all(visual_values[0], 'img', split_axis=1, concat_axis=0, tile...]
    reshape x4 -> x0, local copies, waits for them, and re-layouts: 19.4 us -> none  [the longest x2 10.8 us: latent_terms(): return (key_part.reshape(count, -1), value_part.reshape(count, -1))]
    all_to_all x1 -> x0, waiting for transfers between devices: 15.4 us -> none  [shards(): lax.all_to_all(visual_keys[0], 'img', split_axis=1, concat_axis=0, tiled=...]
    sub x1 -> x0, matrix products: 14.4 us -> none  [attention_grads(): exponent = jnp.where(allowed[None], jnp.exp(masked - row_max), 0.0)]
    all_to_all x4 -> x0, local copies, waits for them, and re-layouts: 13.1 us -> none  [the longest x2 7.28 us: shards(): lax.all_to_all(visual_values[0], 'img', split_axis=1, concat_axis=0, tile...]
  transfers between devices with their start and end apart: 3 -> 0, of which waited for: 3 -> 0; matrix products, arithmetic and copies ran while one was open for 23% -> 0% of each run, Pallas kernels for 0% -> 0%
where the time goes in v1:
time: 87.5 us; the launch traced here: 87.3 us
  Pallas kernels  79 us (90%)
  local copies, waits for them, and re-layouts  7.68 us (9%)
    pallas_call x1, Pallas kernels, attention(): pl.pallas_call(functools.partial(kernel, images_n, sides), grid=(heads,),...  79 us
    unnamed x7, local copies, waits for them, and re-layouts  5.24 us

profile of v1, /device:TPU:0, one launch (start us, length us, event | category | flops | bytes accessed | tf_op | source)
XLA Modules:
  0.0 87.3 jit_solution(2992649710470254738)
XLA Ops:
  0.6 1.2 %tanh_bitcast_fusion.factor_ref = f32[16]{0:T(128)} fusion(f32[1,16]{1,0:T(1,128)} %param.11), kind=kLoop, calls=%fused_computation | loop fusion | bytes 128 | tf_op jit(solution)/shard_map/tanh | solution.py:204
  1.8 1.3 %broadcast_in_dim.12.seen_ref = s32[1,640]{1,0:T(1,128)} reshape(s32[640]{0:T(1024)} %param.13) | data formatting | bytes 5120 | tf_op jit(solution)/shard_map/broadcast_in_dim | solution.py:206
  3.1 79.0 %shard_map.94 = (bf16[640,2048]{1,0:T(8,128)(2,1)}, f32[64,2048]{1,0:T(8,128)}, f32[64,2048]{1,0:T(8,128)}) custom-call(s32[8]{0:T(128)} %bitcast.17, f32[16]{0:T(128)} %tanh_bitcast_fusion.factor_ref, s32[1,640]{1,0:T(1,128)} %broadcast_in_dim.12.seen_ref, bf16[640,2048]{1,0:T(8,128)(2,1)} %bitcast.11, bf16[640,2048]{1,0:T(8,128)(2,1)} %bitcast.12, ...), custom_call_target="tpu_custom_call" | custom-call | tf_op jit(solution)/shard_map/pallas_call | solution.py:180
  82.1 0.0 copy-start.1
  82.1 0.0 copy-start
  82.1 3.6 %copy.13 = bf16[1,640,2048]{2,1,0:T(8,128)(2,1)} copy(bf16[1,640,2048]{2,1,0:T(8,128)(2,1)} %bitcast.10) | data formatting | bytes 5242880
  85.7 0.0 copy-done.1
  85.7 0.8 copy.14
  86.5 0.0 copy-done
  86.5 0.8 copy.15
Async XLA Ops:
  82.1 3.7 %copy-start.1 = (f32[64,2048]{1,0:T(8,128)S(1)}, f32[64,2048]{1,0:T(8,128)}, u32[]{:S(2)}) copy-start(f32[64,2048]{1,0:T(8,128)} %get-tuple-element.7) | copy-start | bytes 1572868
  82.1 4.5 %copy-start = (f32[64,2048]{1,0:T(8,128)S(1)}, f32[64,2048]{1,0:T(8,128)}, u32[]{:S(2)}) copy-start(f32[64,2048]{1,0:T(8,128)} %get-tuple-element.8) | copy-start | bytes 1572868

commit v2 on v1

--- a/solution.py
+++ b/solution.py
@@ -35,7 +35,7 @@
     return query_grad, key_grad, value_grad
 
 
-def kernel(images_n, sides, order_ref, factor_ref, seen_ref, query_ref, grad_ref, key_ref, value_ref,
+def kernel(images_n, sides, order_ref, gate_ref, seen_ref, query_ref, grad_ref, key_ref, value_ref,
            out_ref, key_out, value_out,
            bias, latents, part, pair_out, pair_in, far_out, far_in,
            latent_send, latent_recv, pair_send, pair_recv, far_send, far_recv):
@@ -97,8 +97,9 @@
             return carry
 
         lax.fori_loop(0, heads, send, 0)
-        for i in range(order_ref.shape[0]):
-            bias[pl.ds(i, 1), :] = jnp.where(seen_ref[...] > order_ref[i], 0.0, -1e30)
+        seen = seen_ref[...].reshape(1, bias.shape[1])
+        for i in range(order_ref.shape[1]):
+            bias[pl.ds(i, 1), :] = jnp.where(seen > order_ref[0, i], 0.0, -1e30)
 
     def relay(index):
         pair_copy(index).wait_recv()
@@ -126,7 +127,9 @@
             out[:, columns(index)] = total
 
     drain(latents.at[head], latent_recv.at[head])
-    gated = (grad_ref[...].astype(jnp.float32) * factor_ref[head]).astype(jnp.bfloat16)
+    lane = lax.broadcasted_iota(jnp.int32, gate_ref.shape, 1)
+    gate = jnp.sum(jnp.where(lane == head, gate_ref[...], 0.0), axis=1, keepdims=True)
+    gated = (grad_ref[...].astype(jnp.float32) * jnp.tanh(gate)).astype(jnp.bfloat16)
     query_grad, key_grad, value_grad = head_grads(
         query_ref[...], gated, latents[head, 0], latents[head, 1], bias[...]
     )
@@ -163,9 +166,9 @@
         lax.fori_loop(0, heads, settle, 0)
 
 
-def attention(images_n, texts_n, order, factor, seen, query, grad, key, value):
+def attention(images_n, texts_n, order, gate, seen, query, grad, key, value):
     tokens, width = query.shape
-    heads = factor.shape[0]
+    heads = gate.shape[1]
     head_width = width // heads
     owned = key.shape[0]
     rows = owned * images_n
@@ -180,12 +183,13 @@
     return pl.pallas_call(
         functools.partial(kernel, images_n, sides),
         grid=(heads,),
-        in_specs=[smem, smem, pl.BlockSpec((1, tokens), lambda h: (0, 0)), column, column, hbm, hbm],
+        in_specs=[smem, pl.BlockSpec((1, heads), lambda h: (0, 0)),
+                  pl.BlockSpec((tokens,), lambda h: (0,)), column, column, hbm, hbm],
         out_specs=[column, fixed, fixed],
         out_shape=[jax.ShapeDtypeStruct((tokens, width), half)]
         + [jax.ShapeDtypeStruct((share, width), jnp.float32)] * 2,
         scratch_shapes=[
-            pltpu.VMEM((order.shape[0], tokens), jnp.float32),
+            pltpu.VMEM((order.shape[1], tokens), jnp.float32),
             pltpu.VMEM((heads, 2, rows, head_width), half),
             pltpu.VMEM((2, 2, texts_n, share, head_width), jnp.float32),
             pltpu.VMEM((heads, 2, sides, share, head_width), half),
@@ -197,13 +201,12 @@
         compiler_params=pltpu.CompilerParams(
             vmem_limit_bytes=56 * 1024 * 1024, collective_id=0, has_side_effects=True
         ),
-    )(order, factor, seen, query, grad, key, value)
+    )(order, gate, seen, query, grad, key, value)
 
 
 def shards(images_n, texts_n, queries, visual_keys, visual_values, out_grad, gate_value, image_order, image_seen):
-    factor = jnp.tanh(gate_value[0])
     query_grad, key_share, value_share = attention(
-        images_n, texts_n, image_order[0], factor, image_seen[None, :],
+        images_n, texts_n, image_order, gate_value, image_seen,
         queries[0], out_grad[0], visual_keys[0], visual_values[0]
     )
     return (query_grad[None], key_share[None], value_share[None])

time: 87.5 us -> 84.9 us (0.970)
  local copies, waits for them, and re-layouts: 7.68 us -> 5.24 us
    broadcast_in_dim x1 -> x0, local copies, waits for them, and re-layouts: 1.27 us -> none  [shards(): image_seen[None, :]]
    tanh x1 -> x0, local copies, waits for them, and re-layouts: 1.17 us -> none  [shards(): factor = jnp.tanh(gate_value[0])]
where the time goes in v2:
time: 84.9 us; the launch traced here: 84.8 us
  Pallas kernels  78.9 us (93%)
  local copies, waits for them, and re-layouts  5.24 us (6%)
    pallas_call x1, Pallas kernels, attention(): pl.pallas_call(functools.partial(kernel, images_n, sides), grid=(heads,),...  78.9 us
    unnamed x7, local copies, waits for them, and re-layouts  5.24 us

profile of v2, /device:TPU:0, one launch (start us, length us, event | category | flops | bytes accessed | tf_op | source)
XLA Modules:
  0.0 84.8 jit_solution(762893362487167824)
XLA Ops:
  0.6 78.9 %shard_map.94 = (bf16[640,2048]{1,0:T(8,128)(2,1)}, f32[64,2048]{1,0:T(8,128)}, f32[64,2048]{1,0:T(8,128)}) custom-call(s32[1,8]{1,0:T(1,128)} %order_ref.1, f32[1,16]{1,0:T(1,128)} %gate_ref.1, s32[640]{0:T(1024)} %seen_ref.1, bf16[640,2048]{1,0:T(8,128)(2,1)} %bitcast.8, bf16[640,2048]{1,0:T(8,128)(2,1)} %bitcast.9, bf16[128,8192]{1,0:T(8,128)(2,1)} %bitcast.10, ...), custom_call_target="tpu_custom_call" | custom-call | tf_op jit(solution)/shard_map/pallas_call | solution.py:183
  79.5 0.0 copy-start.1
  79.5 0.0 copy-start
  79.6 3.6 %copy.13 = bf16[1,640,2048]{2,1,0:T(8,128)(2,1)} copy(bf16[1,640,2048]{2,1,0:T(8,128)(2,1)} %bitcast.7) | data formatting | bytes 5242880
  83.2 0.0 copy-done.1
  83.2 0.8 copy.14
  84.0 0.0 copy-done
  84.0 0.8 copy.15
Async XLA Ops:
  79.5 3.7 %copy-start.1 = (f32[64,2048]{1,0:T(8,128)S(1)}, f32[64,2048]{1,0:T(8,128)}, u32[]{:S(2)}) copy-start(f32[64,2048]{1,0:T(8,128)} %get-tuple-element.7) | copy-start | bytes 1572868
  79.5 4.5 %copy-start = (f32[64,2048]{1,0:T(8,128)S(1)}, f32[64,2048]{1,0:T(8,128)}, u32[]{:S(2)}) copy-start(f32[64,2048]{1,0:T(8,128)} %get-tuple-element.8) | copy-start | bytes 1572868
